TPU v7x, 32 devices: a whole 2x2x4 slice. The times are simulated.
32 devices in a mesh: dp: 8 (over z, x), cent: 4 (over y, core).
Axes of the slice: x: 2, y: 2, z: 4, core: 2. Of those that a mesh axis runs over, the one named last changes fastest.
Arguments:
- points: float32 [16384, 512], P('dp'), may hold values from -30 to 30
- centroids: float32 [16384, 512], P('cent'), may hold values from -5 to 5
Outputs:
- new_centroids: float32 [16384, 512], P('cent')
All inputs are finite; a program needn't handle non-finite values.
Results may differ from a plain program's by a relative error of at most 0.0061.
Values sent between devices are 32-bit elements; how exact they have to be, the bound alone decides.
A program may use at most 128 MiB of HBM per device.

v0:
```python
import jax
import jax.numpy as jnp
from jax import lax
from jax.sharding import PartitionSpec as P

D = 512


def joined(part, axis, combine):
    gathered = jax.tree.map(lambda a: lax.all_gather(a, axis), part)

    def take(source):
        return jax.tree.map(lambda a: lax.dynamic_index_in_dim(a, source, 0, False), gathered)

    return lax.fori_loop(
        1, lax.axis_size(axis), lambda source, state: combine(state, take(source)), take(0)
    )


def join_stats(first, second):
    high = jnp.maximum(first[0], second[0])
    summed = first[1] * jnp.exp(first[0] - high) + second[1] * jnp.exp(second[0] - high)
    return (high, summed)


def body(points, centroids):
    point_half = points.astype(jnp.bfloat16)
    cent_half = centroids.astype(jnp.bfloat16)
    sq_norm = jnp.sum(centroids * centroids, axis=1)
    scale = 1.0 / jnp.sqrt(jnp.float32(D))
    inner = lax.dot_general(
        point_half, cent_half, (((1,), (1,)), ((), ())), preferred_element_type=jnp.float32
    )
    logit = (2.0 * inner - sq_norm[None, :]) * scale
    local_top = jnp.max(logit, axis=1)
    local_expo = jnp.exp(logit - local_top[:, None])
    local_total = jnp.sum(local_expo, axis=1)
    top, total = joined((local_top, local_total), "cent", join_stats)
    expo = local_expo * jnp.exp(local_top - top)[:, None]
    resp = (expo / total[:, None]).astype(jnp.bfloat16)
    weighted = lax.dot_general(
        resp, point_half, (((0,), (0,)), ((), ())), preferred_element_type=jnp.float32
    )
    counts = jnp.sum(resp, axis=0, dtype=jnp.float32)
    summed, counted = lax.psum((weighted, counts), "dp")
    return (summed + centroids) / (counted + 1.0)[:, None]


def solution(mesh):
    placed = (P("dp", None), P("cent", None))
    return jax.shard_map(
        body, mesh=mesh, in_specs=placed, out_specs=P("cent", None), check_vma=False
    )
```

profile of v0, /device:TPU:20, one launch (start us, length us, event | category | flops | bytes accessed | tf_op | source)
XLA Modules:
  0.0 374.9 jit_solution(1380463936501937319)
XLA Ops:
  6.5 0.0 all-reduce.2.cloned.1.call-start
  6.5 4.0 %multiply_reduce_fusion = f32[4096]{0:T(1024)S(1)} fusion(f32[4096,512]{1,0:T(8,128)} %param.5), kind=kLoop, calls=%fused_computation.10 | loop fusion | flops 4190208 | bytes 8404992 | tf_op jit(solution)/shard_map/reduce_sum | solution.py:29
  10.5 19.2 %fusion.1 = (f32[2048]{0:T(1024)S(1)}, f32[2048,4096]{1,0:T(8,128)}) fusion(f32[4096]{0:T(1024)S(1)} %multiply_reduce_fusion, f32[4096,512]{1,0:T(8,128)} %param.5, f32[2048,512]{1,0:T(8,128)} %param.4), kind=kOutput, calls=%fused_computation.8 | convolution fusion | flops 8626632704 | bytes 46161920 | tf_op jit(solution)/shard_map/dot_general | solution.py:31
  29.8 15.1 %fusion = f32[2048]{0:T(1024)S(1)} fusion(f32[2048,4096]{1,0:T(8,128)} %get-tuple-element.157, f32[2048]{0:T(1024)S(1)} %get-tuple-element.156, f32[4096]{0:T(1024)S(1)} %multiply_reduce_fusion), kind=kLoop, calls=%fused_computation.7 | loop fusion | flops 41940992 | bytes 33587200 | tf_op jit(solution)/shard_map/reduce_sum | solution.py:37
  44.8 5.2 %all-gather.1 = f32[8192]{0:T(1024)S(1)} all-gather(f32[2048]{0:T(1024)S(1)} %fusion), channel_id=3, replica_groups=mesh['dp'=8,'cent'=4] {'cent'}, dimensions={0}, use_global_device_ids=true | all-gather | bytes 40960 | tf_op jit(solution)/shard_map/all_gather | solution.py:10
  50.1 5.4 %all-gather = f32[8192]{0:T(1024)S(1)} all-gather(f32[2048]{0:T(1024)S(1)} %get-tuple-element.156), channel_id=2, replica_groups=mesh['dp'=8,'cent'=4] {'cent'}, dimensions={0}, use_global_device_ids=true | all-gather | bytes 40960 | tf_op jit(solution)/shard_map/all_gather | solution.py:10
  55.4 0.2 while.17
  55.7 17.1 %convert_reduce_fusion = (f32[4096]{0:T(1024)S(1)}, bf16[2048,4096]{1,0:T(8,128)(2,1)S(1)}) fusion(f32[2048]{0:T(1024)S(1)} %get-tuple-element.139, f32[2048]{0:T(1024)S(1)} %subtract_exponential_fusion.1, f32[2048]{0:T(1024)S(1)} %get-tuple-element.156, f32[4096]{0:T(1024)S(1)} %multiply_reduce_fusion, f32[2048,4096]{1,0:T(8,128)} %get-tuple-element.157), kind=kLoop, calls=%fused_computation.3 | loop fusion | flops 75493376 | bytes 50388992 | tf_op jit(solution)/shard_map/reduce_sum | solution.py:44
  72.8 14.6 %fusion.4 = f32[4096,512]{1,0:T(8,128)} fusion(bf16[2048,4096]{1,0:T(8,128)(2,1)S(1)} %get-tuple-element.153, f32[2048,512]{1,0:T(8,128)} %param.4), kind=kOutput, calls=%fused_computation.13 | convolution fusion | flops 8590983168 | bytes 29360128 | tf_op jit(solution)/shard_map/dot_general | solution.py:41
  87.4 0.0 all-reduce.2.cloned.1.call-update
  87.4 34.4 %psum.15 = f32[4096]{0:T(1024)S(1)} all-reduce(f32[4096]{0:T(1024)S(1)} %get-tuple-element.152), channel_id=1, replica_groups=mesh['dp'=8,'cent'=4] {'dp'}, use_global_device_ids=true, to_apply=%region_7.8 | all-reduce | flops 4096 | bytes 32768 | tf_op jit(solution)/shard_map/psum | solution.py:45
  121.7 236.4 %all-reduce.2.cloned.1.call-done = f32[4096,512]{1,0:T(8,128)} async-done(((f32[4096,512]{1,0:T(8,128)}), f32[4096,512]{1,0:T(8,128)}) %all-reduce.2.cloned.1.call-update) | async-done | bytes 8388624 | tf_op jit(solution)/shard_map/psum | solution.py:45
  358.2 9.9 %add_divide_fusion = f32[4096,512]{1,0:T(8,128)} fusion(f32[4096,512]{1,0:T(8,128)} %all-reduce.2.cloned.1.call-done, f32[4096,512]{1,0:T(8,128)} %param.5, f32[4096]{0:T(1024)S(1)} %broadcast_add_fusion), kind=kLoop, calls=%fused_computation.9 | loop fusion | flops 4194304 | bytes 25182208 | tf_op jit(solution)/shard_map/div | solution.py:46
  (12 shorter events, 0.1 us)
Async XLA Ops:
  6.5 351.6 %all-reduce.2.cloned.1.call-start = ((), (), s32[]{:S(2)}) async-start(), calls=%async_computation | async-start | bytes 16777216 | tf_op jit(solution)/shard_map/psum | solution.py:45
Sparse Core Ops, SparseCore 0:
  87.5 270.6 all-reduce.1
where the time goes:
time: 378 us; the launch traced here: 375 us
  waiting for transfers between devices  236 us (62%)
  other arithmetic  46.1 us (12%)
  blocking collectives  44.9 us (12%)
  matrix products  33.8 us (9%)
  between operations  13.4 us (4%)
    psum x1, waiting for transfers between devices, body(): summed, counted = lax.psum((weighted, counts), 'dp')  236 us
    psum x1, blocking collectives, body(): summed, counted = lax.psum((weighted, counts), 'dp')  34.4 us
    dot_general x1, matrix products, body(): lax.dot_general(point_half, cent_half, (((1,), (1,)), ((), ())), preferre...  19.2 us
    reduce_sum x1, other arithmetic, body(): counts = jnp.sum(resp, axis=0, dtype=jnp.float32)  17.1 us
    reduce_sum x1, other arithmetic, body(): local_total = jnp.sum(local_expo, axis=1)  15.1 us
    dot_general x1, matrix products, body(): lax.dot_general(resp, point_half, (((0,), (0,)), ((), ())), preferred_ele...  14.6 us
    all_gather x2, blocking collectives, joined(): gathered = jax.tree.map(lambda a: lax.all_gather(a, axis), part)  10.6 us
    div x1, other arithmetic, body(): return (summed + centroids) / (counted + 1.0)[:, None]  9.9 us
  transfers between devices with their start and end apart: 1, of which 1 were waited for; matrix products, arithmetic and copies ran while one was open for 0% of the time, Pallas kernels for 0%

commit v1 on v0

v1 whole, which is shorter than its diff:
```python
import functools

import jax
import jax.numpy as jnp
from jax import lax
from jax.experimental import pallas as pl
from jax.experimental.pallas import tpu as pltpu
from jax.sharding import PartitionSpec as P

MESH = pl.DeviceIdType.MESH
LANES = 128
LAG = 2
LOG2E = 1.4426950408889634


def kernel(
    ndp, ncent, geo, pts_ref, cen_ref, out_ref,
    pown, precv, ph, cenf, cenh, bias, ybuf, expo, stats, scale_ref,
    part, recv, final, cnt_part, cnt_recv, cnt_col,
    load_sem, pt_recv, px_send, py_send, pc_send, st_send, st_recv,
    rs_send, rs_recv, cn_send, cn_recv, ag_send, ag_recv, xp_send, xp_recv, out_sem,
):
    rows, half, pb, sub, kb, mb, chunk = geo
    width = pts_ref.shape[1]
    chain = ndp // 2
    last = chain - 1
    dirs = half // 2
    count = dirs // chunk
    share = rows // ncent
    nsub = share // sub
    nblk = share // pb
    per = pb // sub
    nrow = 2 * rows // LANES

    me = lax.axis_index("dp")
    cent = lax.axis_index("cent")
    z, x = me // 2, lax.rem(me, 2)
    core, yy = lax.rem(cent, 2), cent // 2
    other = z * 2 + (1 - x)
    mate = yy * 2 + (1 - core)
    mine = x * ncent + cent

    def remote(src, dst, send, got, dp, ce):
        return pltpu.make_async_remote_copy(
            src_ref=src, dst_ref=dst, send_sem=send, recv_sem=got,
            device_id=(dp, ce), device_id_type=MESH,
        )

    load_p = pltpu.make_async_copy(pts_ref, pown, load_sem.at[0])
    load_c = pltpu.make_async_copy(
        cen_ref.at[pl.ds(pl.multiple_of(x * half, half), half)], cenf, load_sem.at[1]
    )
    load_p.start()
    load_c.start()
    load_p.wait()

    def span(owner, j):
        return pl.ds(pl.multiple_of(owner * share + j * sub, sub), sub)

    swaps = []
    for j in range(nsub):
        copy = remote(
            pown.at[span(cent, j)], precv.at[span(cent, j)],
            px_send.at[j], pt_recv.at[cent * nsub + j], other, cent,
        )
        copy.start()
        swaps.append(copy)
    load_c.wait()

    root = jnp.float32(1.0) / jnp.sqrt(jnp.float32(width))
    gain = 2.0 * root * LOG2E
    norm_gain = root * LOG2E

    def prepare(k, carry):
        at = pl.ds(pl.multiple_of(k * mb, mb), mb)
        c = cenf[at, :]
        cenh[at, :] = c.astype(jnp.bfloat16)
        bias[at, :] = jnp.broadcast_to(
            jnp.sum(c * c, axis=1, keepdims=True) * norm_gain, (mb, LANES)
        )
        return carry

    lax.fori_loop(0, half // mb, prepare, 0)

    def block(src, row, col):
        pv = src[pl.ds(pl.multiple_of(row, pb), pb), :].astype(jnp.bfloat16)
        cols = pl.ds(pl.multiple_of(col, pb), pb)
        ph[cols, :] = pv

        def logits(k, top):
            at = pl.ds(pl.multiple_of(k * kb, kb), kb)
            inner = lax.dot_general(
                cenh[at, :], pv, (((1,), (1,)), ((), ())), preferred_element_type=jnp.float32
            )
            b = bias[at, :]
            y = inner * gain - jnp.concatenate([b] * (pb // LANES), axis=1)
            ybuf[at, :] = y
            return jnp.maximum(top, jnp.max(y, axis=0, keepdims=True))

        top = lax.fori_loop(
            0, half // kb, logits, jnp.full((1, pb), -jnp.inf, jnp.float32)
        )

        def powers(k, total):
            at = pl.ds(pl.multiple_of(k * kb, kb), kb)
            e = jnp.exp2(ybuf[at, :] - top)
            expo[at, cols] = e.astype(jnp.bfloat16)
            return total + jnp.sum(e, axis=0, keepdims=True)

        total = lax.fori_loop(0, half // kb, powers, jnp.zeros((1, pb), jnp.float32))
        base = col // LANES
        for h in range(pb // LANES):
            stats[mine, pl.ds(base + h, 1), :] = top[:, h * LANES:(h + 1) * LANES]
            stats[mine, pl.ds(nrow + base + h, 1), :] = total[:, h * LANES:(h + 1) * LANES]

    def own(b, carry):
        block(pown, b * pb, x * rows + b * pb)
        return carry

    lax.fori_loop(0, rows // pb, own, 0)

    sends = []

    def arrived(owner, j):
        remote(
            precv.at[span(owner, j)], precv.at[span(owner, j)],
            px_send.at[0], pt_recv.at[owner * nsub + j], other, cent,
        ).wait_recv()

    def forward(owner, j, dp, ce, sem):
        copy = remote(
            precv.at[span(owner, j)], precv.at[span(owner, j)],
            sem, pt_recv.at[owner * nsub + j], dp, ce,
        )
        copy.start()
        sends.append(copy)

    ny = ncent // 2
    same = [lax.rem(yy + d, ny) * 2 + core for d in range(1, ny)]
    cross = [lax.rem(yy + d, ny) * 2 + (1 - core) for d in range(1, ny)]

    def theirs(owner, b, wait):
        if wait:
            for j in range(per):
                arrived(owner, b * per + j)
        row = owner * share + b * pb
        block(precv, row, (1 - x) * rows + row)

    for j in range(nsub + 1):
        if j < nsub:
            arrived(cent, j)
            for i, d in enumerate(same):
                forward(cent, j, me, d, py_send.at[i * nsub + j])
            forward(cent, j, me, mate, pc_send.at[j])
        if j >= 1:
            for i, d in enumerate(same):
                arrived(d, j - 1)
                forward(d, j - 1, me, mate, pc_send.at[(i + 1) * nsub + j - 1])
        if j < nsub and j % per == per - 1:
            theirs(cent, j // per, False)
        if j >= 1 and (j - 1) % per == per - 1:
            theirs(mate, (j - 1) // per, True)
    for b in range(nblk):
        for d in same:
            theirs(d, b, False)
        for d in cross:
            theirs(d, b, True)

    group = 2 * ncent
    stat_sends = []
    for o in range(1, group):
        peer = lax.rem(mine + o, group)
        copy = remote(
            stats.at[mine], stats.at[mine], st_send.at[o], st_recv.at[mine],
            z * 2 + peer // ncent, lax.rem(peer, ncent),
        )
        copy.start()
        stat_sends.append(copy)
    for o in range(1, group):
        peer = lax.rem(mine + o, group)
        remote(
            stats.at[peer], stats.at[peer], st_send.at[o], st_recv.at[peer], other, cent
        ).wait_recv()
    high = stats[0, 0:nrow, :]
    for s in range(1, group):
        high = jnp.maximum(high, stats[s, 0:nrow, :])
    summed = jnp.zeros((nrow, LANES), jnp.float32)
    for s in range(group):
        summed = summed + stats[s, nrow:, :] * jnp.exp2(stats[s, 0:nrow, :] - high)
    scale_ref[...] = jnp.exp2(stats[mine, 0:nrow, :] - high) / summed

    def place(d):
        return z if d == 0 else last - z

    def ahead(d):
        return (z + 1 if d == 0 else z - 1) * 2 + x

    def behind(d):
        return (z - 1 if d == 0 else z + 1) * 2 + x

    def crows(d, i):
        return pl.ds(pl.multiple_of(d * dirs + i * chunk, chunk), chunk)

    pair = LANES // chunk
    ncnt = count // pair

    def pass_on(d, i, src, cnt):
        remote(
            src.at[crows(d, i)], recv.at[crows(d, i)],
            rs_send.at[d], rs_recv.at[d * count + i], ahead(d), cent,
        ).start()

        @pl.when(lax.rem(i, pair) == 0)
        def _():
            slot = d * ncnt + i // pair
            remote(
                cnt.at[slot], cnt_recv.at[slot], cn_send.at[d], cn_recv.at[slot], ahead(d), cent
            ).start()

    def weigh(d, j):
        at = pl.ds(pl.multiple_of(d * dirs + j * mb, mb), mb)

        def rescale(q, acc):
            cols = pl.ds(pl.multiple_of(q * LANES, LANES), LANES)
            r = expo[at, cols].astype(jnp.float32) * scale_ref[pl.ds(q, 1), :]
            r = r.astype(jnp.bfloat16)
            expo[at, cols] = r
            return acc + r.astype(jnp.float32)

        acc = lax.fori_loop(0, nrow, rescale, jnp.zeros((mb, LANES), jnp.float32), unroll=2)
        for h in range(mb // LANES):
            line = jnp.sum(acc[h * LANES:(h + 1) * LANES, :].T, axis=0, keepdims=True)
            cnt_part[d * ncnt + j * (mb // LANES) + h] = jnp.broadcast_to(line, (8, LANES))
        part[at, :] = jnp.dot(expo[at, :], ph[...], preferred_element_type=jnp.float32)

        for which in (0, 1):
            @pl.when(jnp.logical_and(d == which, place(which) == 0))
            def _():
                for i in range(mb // chunk):
                    pass_on(which, j * (mb // chunk) + i, part, cnt_part)

    def both(t, carry):
        first = jnp.where(z < chain // 2, 0, 1)
        d = lax.rem(first + lax.rem(t, 2), 2)
        weigh(d, t // 2)
        return carry

    lax.fori_loop(0, 2 * (dirs // mb), both, 0)

    def hand_out(d, i):
        rows_out = pl.ds(pl.multiple_of(x * half + d * dirs + i * chunk, chunk), chunk)
        src = final.at[crows(d, i)]
        remote(src, out_ref.at[rows_out], xp_send.at[d], xp_recv.at[d], other, cent).start()
        pltpu.make_async_copy(src, out_ref.at[rows_out], out_sem.at[d]).start()

        @pl.when(place(d) > 0)
        def _():
            remote(
                src, src, ag_send.at[d], ag_recv.at[d * count + i], behind(d), cent
            ).start()

    def tick(t, carry):
        for d in (0, 1):
            pos = place(d)
            i = t - LAG * pos

            @pl.when((pos > 0) & (i >= 0) & (i < count))
            def _():
                at = crows(d, i)
                slot = d * ncnt + i // pair
                remote(
                    recv.at[at], recv.at[at], rs_send.at[d], rs_recv.at[d * count + i], other, cent
                ).wait_recv()

                @pl.when(lax.rem(i, pair) == 0)
                def _():
                    remote(
                        cnt_recv.at[slot], cnt_recv.at[slot],
                        cn_send.at[d], cn_recv.at[slot], other, cent,
                    ).wait_recv()

                @pl.when(pos < last)
                def _():
                    recv[at, :] = recv[at, :] + part[at, :]

                    @pl.when(lax.rem(i, pair) == 0)
                    def _():
                        cnt_recv[slot] = cnt_recv[slot] + cnt_part[slot]

                    pass_on(d, i, recv, cnt_recv)

                @pl.when(pos == last)
                def _():
                    @pl.when(lax.rem(i, pair) == 0)
                    def _():
                        line = cnt_recv[slot] + cnt_part[slot] + 1.0
                        cnt_col[d] = jnp.broadcast_to(line[0:1, :], (LANES, LANES)).T

                    div = cnt_col[d, pl.ds(pl.multiple_of(lax.rem(i, pair) * chunk, chunk), chunk), :]
                    div = jnp.concatenate([div] * (width // LANES), axis=1)
                    final[at, :] = (recv[at, :] + part[at, :] + cenf[at, :]) / div
                    hand_out(d, i)

        for d in (0, 1):
            pos = place(d)
            i = t - LAG * (2 * last - pos)

            @pl.when((pos < last) & (i >= 0) & (i < count))
            def _():
                at = crows(d, i)
                remote(
                    final.at[at], final.at[at], ag_send.at[d], ag_recv.at[d * count + i], other, cent
                ).wait_recv()
                hand_out(d, i)

        return carry

    lax.fori_loop(0, count + LAG * 2 * last, tick, 0)

    for copy in swaps + sends + stat_sends:
        copy.wait_send()
    for d in (0, 1):
        at = pl.ds(d * dirs, dirs)
        cs = pl.ds(d * ncnt, ncnt)

        @pl.when(place(d) < last)
        def _():
            remote(recv.at[at], recv.at[at], rs_send.at[d], rs_recv.at[0], other, cent).wait_send()
            remote(
                cnt_recv.at[cs], cnt_recv.at[cs], cn_send.at[d], cn_recv.at[0], other, cent
            ).wait_send()

        @pl.when(place(d) > 0)
        def _():
            remote(final.at[at], final.at[at], ag_send.at[d], ag_recv.at[0], other, cent).wait_send()

        here = pl.ds(pl.multiple_of(x * half + d * dirs, dirs), dirs)
        there = pl.ds(pl.multiple_of((1 - x) * half + d * dirs, dirs), dirs)
        pltpu.make_async_copy(final.at[at], out_ref.at[here], out_sem.at[d]).wait()
        remote(final.at[at], out_ref.at[there], xp_send.at[d], xp_recv.at[d], other, cent).wait()


def body(ndp, ncent, points, centroids):
    rows, width = points.shape
    half = centroids.shape[0] // 2
    share = rows // ncent
    pb = min(256, share)
    sub = pb // 2
    kb, mb, chunk = 512, 256, 64
    dirs = half // 2
    count = dirs // chunk
    ncnt = dirs // LANES
    nsub = share // sub
    ny = ncent // 2
    nrow = 2 * rows // LANES
    f32, bf16 = jnp.float32, jnp.bfloat16
    dma = pltpu.SemaphoreType.DMA
    return pl.pallas_call(
        functools.partial(kernel, ndp, ncent, (rows, half, pb, sub, kb, mb, chunk)),
        out_shape=jax.ShapeDtypeStruct(centroids.shape, f32),
        in_specs=[pl.BlockSpec(memory_space=pl.ANY)] * 2,
        out_specs=pl.BlockSpec(memory_space=pl.ANY),
        scratch_shapes=[
            pltpu.VMEM((rows, width), f32),
            pltpu.VMEM((rows, width), f32),
            pltpu.VMEM((2 * rows, width), bf16),
            pltpu.VMEM((half, width), f32),
            pltpu.VMEM((half, width), bf16),
            pltpu.VMEM((half, LANES), f32),
            pltpu.VMEM((half, pb), f32),
            pltpu.VMEM((half, 2 * rows), bf16),
            pltpu.VMEM((2 * ncent, 2 * nrow, LANES), f32),
            pltpu.VMEM((nrow, LANES), f32),
            pltpu.VMEM((half, width), f32),
            pltpu.VMEM((half, width), f32),
            pltpu.VMEM((half, width), f32),
            pltpu.VMEM((2 * ncnt, 8, LANES), f32),
            pltpu.VMEM((2 * ncnt, 8, LANES), f32),
            pltpu.VMEM((2, LANES, LANES), f32),
            dma((2,)),
            dma((ncent * nsub,)),
            dma((nsub,)),
            dma(((ny - 1) * nsub,)),
            dma((ny * nsub,)),
            dma((2 * ncent,)),
            dma((2 * ncent,)),
            dma((2,)),
            dma((2 * count,)),
            dma((2,)),
            dma((2 * ncnt,)),
            dma((2,)),
            dma((2 * count,)),
            dma((2,)),
            dma((2,)),
            dma((2,)),
        ],
        compiler_params=pltpu.CompilerParams(
            has_side_effects=True, vmem_limit_bytes=63 * 2**20
        ),
        name="kmeans",
    )(points, centroids)


def solution(mesh):
    placed = (P("dp", None), P("cent", None))
    return jax.shard_map(
        functools.partial(body, mesh.shape["dp"], mesh.shape["cent"]),
        mesh=mesh, in_specs=placed, out_specs=P("cent", None), check_vma=False,
    )
```

time: 378 us -> 217 us (0.57)
  waiting for transfers between devices: 236 us -> 0 us
  Pallas kernels: 0 us -> 209 us
  other arithmetic: 46.1 us -> 0 us
  blocking collectives: 44.9 us -> 0 us
  matrix products: 33.8 us -> 0 us
  between operations: 13.4 us -> 0.01 us
  local copies, waits for them, and re-layouts: 0.09 us -> 7.76 us
    psum x1 -> x0, waiting for transfers between devices: 236 us -> none  [body(): summed, counted = lax.psum((weighted, counts), 'dp')]
    pallas_call x0 -> x1, Pallas kernels: none -> 209 us  [body(): pl.pallas_call(functools.partial(kernel, ndp, ncent, (rows, half, pb, sub...]
    reduce_sum x3 -> x0, other arithmetic: 36.2 us -> none  [the longest x1 17.1 us: body(): counts = jnp.sum(resp, axis=0, dtype=jnp.float32)]
    psum x1 -> x0, blocking collectives: 34.4 us -> none  [body(): summed, counted = lax.psum((weighted, counts), 'dp')]
    dot_general x2 -> x0, matrix products: 33.8 us -> none  [the longest x1 19.2 us: body(): lax.dot_general(point_half, cent_half, (((1,), (1,)), ((), ())), preferre...]
    all_gather x2 -> x0, blocking collectives: 10.6 us -> none  [joined(): gathered = jax.tree.map(lambda a: lax.all_gather(a, axis), part)]
    div x1 -> x0, other arithmetic: 9.9 us -> none  [body(): return (summed + centroids) / (counted + 1.0)[:, None]]
    unnamed x0 -> x1, local copies, waits for them, and re-layouts: none -> 7.76 us
  transfers between devices with their start and end apart: 1 -> 0, of which waited for: 1 -> 0; matrix products, arithmetic and copies ran while one was open for 0% -> 0% of each run, Pallas kernels for 0% -> 0%
where the time goes in v1:
time: 217 us; the launch traced here: 216 us
  Pallas kernels  209 us (96%)
  local copies, waits for them, and re-layouts  7.76 us (4%)
    pallas_call x1, Pallas kernels, body(): pl.pallas_call(functools.partial(kernel, ndp, ncent, (rows, half, pb, sub...  209 us
    unnamed x1, local copies, waits for them, and re-layouts  7.76 us

profile of v1, /device:TPU:20, one launch (start us, length us, event | category | flops | bytes accessed | tf_op | source)
XLA Modules:
  0.0 216.4 jit_solution(15052007406894423998)
XLA Ops:
  0.0 208.6 %kmeans.1 = f32[4096,512]{1,0:T(8,128)} custom-call(f32[2048,512]{1,0:T(8,128)} %pts_ref.1, f32[4096,512]{1,0:T(8,128)} %cen_ref.1), custom_call_target="tpu_custom_call" | custom-call | tf_op jit(solution)/shard_map/kmeans/pallas_call | solution.py:358
  208.6 7.8 %copy.4 = f32[4096,512]{1,0:T(8,128)} copy(f32[4096,512]{1,0:T(8,128)} %kmeans.1) | data formatting | bytes 16777216

commit v2 on v1

--- a/solution.py
+++ b/solution.py
@@ -52,6 +52,25 @@
     )
     load_p.start()
     load_c.start()
+
+    barrier = pltpu.get_barrier_semaphore()
+    for o in range(1, 2 * ncent):
+        peer = lax.rem(mine + o, 2 * ncent)
+        pl.semaphore_signal(
+            barrier, inc=1, device_id=(z * 2 + peer // ncent, lax.rem(peer, ncent)),
+            device_id_type=MESH,
+        )
+
+    @pl.when(z > 0)
+    def _():
+        pl.semaphore_signal(barrier, inc=1, device_id=(me - 2, cent), device_id_type=MESH)
+
+    @pl.when(z < last)
+    def _():
+        pl.semaphore_signal(barrier, inc=1, device_id=(me + 2, cent), device_id_type=MESH)
+
+    ends = jnp.where(z > 0, 1, 0) + jnp.where(z < last, 1, 0)
+    pl.semaphore_wait(barrier, 2 * ncent - 1 + ends)
     load_p.wait()
 
     def span(owner, j):
@@ -98,7 +117,7 @@
             return jnp.maximum(top, jnp.max(y, axis=0, keepdims=True))
 
         top = lax.fori_loop(
-            0, half // kb, logits, jnp.full((1, pb), -jnp.inf, jnp.float32)
+            0, half // kb, logits, jnp.full((1, pb), -jnp.inf, jnp.float32), unroll=True
         )
 
         def powers(k, total):
@@ -107,7 +126,7 @@
             expo[at, cols] = e.astype(jnp.bfloat16)
             return total + jnp.sum(e, axis=0, keepdims=True)
 
-        total = lax.fori_loop(0, half // kb, powers, jnp.zeros((1, pb), jnp.float32))
+        total = lax.fori_loop(0, half // kb, powers, jnp.zeros((1, pb), jnp.float32), unroll=True)
         base = col // LANES
         for h in range(pb // LANES):
             stats[mine, pl.ds(base + h, 1), :] = top[:, h * LANES:(h + 1) * LANES]
@@ -116,8 +135,6 @@
     def own(b, carry):
         block(pown, b * pb, x * rows + b * pb)
         return carry
-
-    lax.fori_loop(0, rows // pb, own, 0)
 
     sends = []
 
@@ -146,7 +163,11 @@
         row = owner * share + b * pb
         block(precv, row, (1 - x) * rows + row)
 
+    nown = rows // pb
+    lax.fori_loop(0, nown // 2, own, 0)
     for j in range(nsub + 1):
+        if j == 1:
+            lax.fori_loop(nown // 2, nown, own, 0)
         if j < nsub:
             arrived(cent, j)
             for i, d in enumerate(same):
@@ -203,6 +224,7 @@
 
     pair = LANES // chunk
     ncnt = count // pair
+    window = LAG * last
 
     def pass_on(d, i, src, cnt):
         remote(
@@ -236,8 +258,12 @@
         for which in (0, 1):
             @pl.when(jnp.logical_and(d == which, place(which) == 0))
             def _():
-                for i in range(mb // chunk):
-                    pass_on(which, j * (mb // chunk) + i, part, cnt_part)
+                for h in range(mb // chunk):
+                    i = j * (mb // chunk) + h
+
+                    @pl.when(i < window)
+                    def _():
+                        pass_on(which, i, part, cnt_part)
 
     def both(t, carry):
         first = jnp.where(z < chain // 2, 0, 1)
@@ -245,8 +271,6 @@
         weigh(d, t // 2)
         return carry
 
-    lax.fori_loop(0, 2 * (dirs // mb), both, 0)
-
     def hand_out(d, i):
         rows_out = pl.ds(pl.multiple_of(x * half + d * dirs + i * chunk, chunk), chunk)
         src = final.at[crows(d, i)]
@@ -263,6 +287,10 @@
         for d in (0, 1):
             pos = place(d)
             i = t - LAG * pos
+
+            @pl.when((pos == 0) & (i >= window) & (i < count))
+            def _():
+                pass_on(d, i, part, cnt_part)
 
             @pl.when((pos > 0) & (i >= 0) & (i < count))
             def _():
@@ -315,7 +343,16 @@
 
         return carry
 
-    lax.fori_loop(0, count + LAG * 2 * last, tick, 0)
+    units = 2 * (dirs // mb)
+    early = max(2, units - window)
+
+    def mixed(t, carry):
+        tick(t, carry)
+        return both(early + t, carry)
+
+    lax.fori_loop(0, early, both, 0)
+    lax.fori_loop(0, units - early, mixed, 0)
+    lax.fori_loop(units - early, count + LAG * 2 * last, tick, 0)
 
     for copy in swaps + sends + stat_sends:
         copy.wait_send()
@@ -345,8 +382,8 @@
     half = centroids.shape[0] // 2
     share = rows // ncent
     pb = min(256, share)
-    sub = pb // 2
-    kb, mb, chunk = 512, 256, 64
+    sub = pb // 4
+    kb, mb, chunk = 512, 256, 32
     dirs = half // 2
     count = dirs // chunk
     ncnt = dirs // LANES
@@ -395,7 +432,7 @@
             dma((2,)),
         ],
         compiler_params=pltpu.CompilerParams(
-            has_side_effects=True, vmem_limit_bytes=63 * 2**20
+            collective_id=0, has_side_effects=True, vmem_limit_bytes=63 * 2**20
         ),
         name="kmeans",
     )(points, centroids)

time: 217 us -> 179 us (0.82)
  Pallas kernels: 209 us -> 171 us
    pallas_call x1, Pallas kernels: 209 us -> 171 us  [body(): pl.pallas_call(functools.partial(kernel, ndp, ncent, (rows, half, pb, sub...]
where the time goes in v2:
time: 179 us; the launch traced here: 178 us
  Pallas kernels  171 us (96%)
  local copies, waits for them, and re-layouts  7.76 us (4%)
    pallas_call x1, Pallas kernels, body(): pl.pallas_call(functools.partial(kernel, ndp, ncent, (rows, half, pb, sub...  171 us
    unnamed x1, local copies, waits for them, and re-layouts  7.76 us

profile of v2, /device:TPU:20, one launch (start us, length us, event | category | flops | bytes accessed | tf_op | source)
XLA Modules:
  0.0 178.3 jit_solution(7015444214761015998)
XLA Ops:
  0.0 170.5 %kmeans.1 = f32[4096,512]{1,0:T(8,128)} custom-call(f32[2048,512]{1,0:T(8,128)} %pts_ref.1, f32[4096,512]{1,0:T(8,128)} %cen_ref.1), custom_call_target="tpu_custom_call" | custom-call | tf_op jit(solution)/shard_map/kmeans/pallas_call | solution.py:395
  170.5 7.8 %copy.4 = f32[4096,512]{1,0:T(8,128)} copy(f32[4096,512]{1,0:T(8,128)} %kmeans.1) | data formatting | bytes 16777216

commit v3 on v2

--- a/solution.py
+++ b/solution.py
@@ -249,7 +249,7 @@
             expo[at, cols] = r
             return acc + r.astype(jnp.float32)
 
-        acc = lax.fori_loop(0, nrow, rescale, jnp.zeros((mb, LANES), jnp.float32), unroll=2)
+        acc = lax.fori_loop(0, nrow, rescale, jnp.zeros((mb, LANES), jnp.float32), unroll=True)
         for h in range(mb // LANES):
             line = jnp.sum(acc[h * LANES:(h + 1) * LANES, :].T, axis=0, keepdims=True)
             cnt_part[d * ncnt + j * (mb // LANES) + h] = jnp.broadcast_to(line, (8, LANES))

time: 179 us -> 168 us (0.939)
  Pallas kernels: 171 us -> 159 us
    pallas_call x1, Pallas kernels: 171 us -> 159 us  [body(): pl.pallas_call(functools.partial(kernel, ndp, ncent, (rows, half, pb, sub...]
where the time goes in v3:
time: 168 us; the launch traced here: 167 us
  Pallas kernels  159 us (95%)
  local copies, waits for them, and re-layouts  7.76 us (5%)
    pallas_call x1, Pallas kernels, body(): pl.pallas_call(functools.partial(kernel, ndp, ncent, (rows, half, pb, sub...  159 us
    unnamed x1, local copies, waits for them, and re-layouts  7.76 us

profile of v3, /device:TPU:20, one launch (start us, length us, event | category | flops | bytes accessed | tf_op | source)
XLA Modules:
  0.0 166.9 jit_solution(4234154988586339905)
XLA Ops:
  0.0 159.2 %kmeans.1 = f32[4096,512]{1,0:T(8,128)} custom-call(f32[2048,512]{1,0:T(8,128)} %pts_ref.1, f32[4096,512]{1,0:T(8,128)} %cen_ref.1), custom_call_target="tpu_custom_call" | custom-call | tf_op jit(solution)/shard_map/kmeans/pallas_call | solution.py:395
  159.2 7.8 %copy.4 = f32[4096,512]{1,0:T(8,128)} copy(f32[4096,512]{1,0:T(8,128)} %kmeans.1) | data formatting | bytes 16777216
